TPU v7x, 32 devices: a whole 2x2x4 slice. The times are simulated.
32 devices in a mesh: row: 4 (over y, x), col: 8 (over z, core).
Axes of the slice: x: 2, y: 2, z: 4, core: 2. Of those that a mesh axis runs over, the one named last changes fastest.
Arguments:
- h_old: float32 [4, 8, 2048, 4096], P('row', 'col'), may hold values from -2 to 2, as said below
- s_old: float32 [4, 8, 2048, 128], P('row', 'col'), may hold values from -100 to 100, as said below
- row_owner: int32 [256], replicated, may hold values from 0 to 7, as said below
- col_owner: int32 [256], replicated, may hold values from 0 to 3, as said below
Outputs:
- h_reduced: float32 [16384, 16384], P('row', 'col')
- panel_factor: float32 [16384, 512], P('row')
Inputs may be any that keep to these rules, and one draw needn't show every extreme that they name: `row_owner`: each aligned run of 8 entries is an ordering of 0 to 7. `col_owner`: each aligned run of 4 entries is an ordering of 0 to 3. `s_old`: the first 512 rows of S_panel form a symmetric positive definite matrix. `h_old`: H is symmetric.
All inputs are finite; a program needn't handle non-finite values.
Results may differ from a plain program's by a relative error of at most 0.00017.
Values sent between devices are 32-bit elements; how exact they have to be, the bound alone decides.
A program may use at most 320 MiB of HBM per device.

v0:
```python
import jax
import jax.numpy as jnp
from jax import lax
from jax.sharding import PartitionSpec as P

ORDER = 16384
PANEL = 512
BLOCK = 64


def broadcast(block, axis, holder):
    block = jnp.where(lax.axis_index(axis) == holder, block, jnp.zeros_like(block))
    return lax.psum(block, axis)


def per_device(h_old, s_old, row_owner, col_owner):
    row_count = lax.axis_size("row")
    col_count = lax.axis_size("col")
    old_rows = 2 * row_count
    old_cols = col_count // 2
    row_id = lax.axis_index("row")
    col_id = lax.axis_index("col")
    local_h = h_old[0, 0]
    local_s = s_old[0, 0]
    rows_here, cols_here = local_h.shape
    part_rows = rows_here // row_count
    part_cols = cols_here // col_count
    band = ORDER // row_count
    strip = ORDER // col_count
    panel_local = local_s.shape[1]
    rounds_row = part_rows // BLOCK
    rounds_col = part_cols // BLOCK
    span_row = rounds_row * old_rows
    span_col = rounds_col * old_cols
    owner_row = lax.dynamic_slice_in_dim(row_owner, row_id * span_row, span_row)[:, None]
    owner_col = lax.dynamic_slice_in_dim(col_owner, col_id * span_col, span_col)[None, :]
    round_row = (jnp.arange(span_row, dtype=jnp.int32) // old_rows)[:, None]
    round_col = (jnp.arange(span_col, dtype=jnp.int32) // old_cols)[None, :]
    outgoing = local_h.reshape(row_count, part_rows, col_count, part_cols).transpose(0, 2, 1, 3)
    received = lax.all_to_all(
        outgoing.reshape(row_count * col_count, part_rows, part_cols),
        ("row", "col"),
        split_axis=0,
        concat_axis=0,
        tiled=True,
    )
    grid_h = received.reshape(row_count, col_count, rounds_row, BLOCK, rounds_col, BLOCK)
    shape_two = (span_row, span_col)
    source_row = jnp.broadcast_to(owner_row // 2, shape_two)
    source_col = 2 * owner_col + owner_row % 2
    picked = grid_h[
        source_row,
        source_col,
        jnp.broadcast_to(round_row, shape_two),
        :,
        jnp.broadcast_to(round_col, shape_two),
        :,
    ]
    h_block = picked.transpose(0, 2, 1, 3).reshape(band, strip)
    panel_blocks = PANEL // BLOCK
    panel_shape = (span_row, panel_blocks)
    panel_owner = col_owner[:panel_blocks][None, :]
    panel_slot = jnp.broadcast_to(
        (jnp.arange(panel_blocks, dtype=jnp.int32) // old_cols)[None, :], panel_shape
    )
    gather_col = 2 * panel_owner + owner_row % 2
    gather_row = jnp.broadcast_to(owner_row // 2, panel_shape)
    gather_round = jnp.broadcast_to(round_row, panel_shape)

    def arrange(gathered):
        grid_panel = gathered.reshape(
            col_count, row_count, rounds_row, BLOCK, panel_local // BLOCK, BLOCK
        )
        chosen = grid_panel[gather_col, gather_row, gather_round, :, panel_slot, :]
        return chosen.transpose(0, 2, 1, 3).reshape(band, PANEL)

    s_pieces = local_s.reshape(row_count, part_rows, panel_local)
    h_pieces = local_h[:, :panel_local].reshape(row_count, part_rows, panel_local)
    s_rows, h_rows = (
        lax.all_to_all(s_pieces, "row", split_axis=0, concat_axis=0, tiled=True),
        lax.all_to_all(h_pieces, "row", split_axis=0, concat_axis=0, tiled=True),
    )
    s_all, h_all = (
        lax.all_gather(s_rows[None], "col", axis=0, tiled=True),
        lax.all_gather(h_rows[None], "col", axis=0, tiled=True),
    )
    s_panel = arrange(s_all)
    h_panel = arrange(h_all)
    corner_s, corner_h = (
        broadcast(s_panel[:PANEL], "row", 0),
        broadcast(h_panel[:PANEL], "row", 0),
    )
    lower_factor = jnp.linalg.cholesky(corner_s)
    solved = lax.linalg.triangular_solve(lower_factor, s_panel.T, left_side=True, lower=True)
    panel_factor = solved.T
    coupling = lax.linalg.triangular_solve(
        lower_factor, solved, left_side=True, lower=True, transpose_a=True
    ).T
    identity = jnp.eye(PANEL, dtype=jnp.float32)
    inverse = lax.linalg.triangular_solve(lower_factor, identity, left_side=True, lower=True)
    top_rows = jnp.concatenate(
        [identity - inverse, jnp.zeros((band - PANEL, PANEL), jnp.float32)], 0
    )
    leading = jnp.logical_and(row_id == 0, jnp.arange(band, dtype=jnp.int32)[:, None] < PANEL)
    coupling = jnp.where(leading, top_rows, coupling)
    mixed = h_panel - 0.5 * jnp.dot(coupling, corner_h, precision=lax.Precision.HIGHEST)
    offset = col_id * strip % band
    root_row = col_id * strip // band
    column_n, column_q = (
        broadcast(lax.dynamic_slice_in_dim(coupling, offset, strip), "row", root_row),
        broadcast(lax.dynamic_slice_in_dim(mixed, offset, strip), "row", root_row),
    )
    left_terms = jnp.concatenate([coupling, mixed], 1)
    right_terms = jnp.concatenate([column_q, column_n], 1)
    update = lax.dot_general(
        left_terms,
        right_terms,
        (((1,), (1,)), ((), ())),
        precision=lax.Precision.HIGHEST,
        preferred_element_type=jnp.float32,
    )
    return (h_block - update, panel_factor)


def solution(mesh):
    in_specs = (P("row", "col", None, None), P("row", "col", None, None), P(), P())
    out_specs = (P("row", "col"), P("row", None))
    return jax.shard_map(
        per_device, mesh=mesh, in_specs=in_specs, out_specs=out_specs, check_vma=False
    )
```

profile of v0, /device:TPU:11, one launch (start us, length us, event | category | flops | bytes accessed | tf_op | source)
XLA Modules:
  0.0 1406.5 jit_solution(13387984591292326987)
XLA Ops:
  9.4 3.7 all-to-all-start.2
  13.2 38.0 %copy.70 = f32[256,8,8,512]{3,2,1,0:T(8,128)} copy(f32[256,8,8,512]{3,1,2,0:T(8,128)} %bitcast.123) | data formatting | bytes 67108864
  51.2 3.6 all-to-all-start.1
  54.8 12.7 bitcast_bitcast_fusion
  67.5 36.4 %copy.43 = f32[4,8,512,512]{3,2,1,0:T(8,128)} copy(f32[4,8,512,512]{3,1,2,0:T(8,128)S(1)} %bitcast_bitcast_fusion) | data formatting | bytes 67108864 | tf_op jit(solution)/shard_map/transpose | solution.py:39
  104.8 7.4 all-to-all-start
  114.6 177.1 %all-gather.7.cloned.1.call-done = f32[32,512,128]{2,1,0:T(8,128)} async-done(((f32[4,512,128]{2,1,0:T(8,128)}), f32[32,512,128]{2,1,0:T(8,128)}) %all-gather.7.cloned.1.call-update) | async-done | bytes 8388624 | tf_op jit(solution)/shard_map/all_gather | solution.py:85
  291.7 16.9 %reshape.675 = f32[8,4,8,64,2,64]{5,4,3,2,1,0:T(2,128)} reshape(f32[32,512,128]{2,1,0:T(8,128)} %all-gather.7.cloned.1.call-done) | data formatting | bytes 16777216 | tf_op jit(solution)/shard_map/reshape | solution.py:71
  308.6 13.4 copy.57
  321.9 210.5 %all-gather.5.cloned.1.call-done = f32[32,512,128]{2,1,0:T(8,128)} async-done(((f32[4,512,128]{2,1,0:T(8,128)}), f32[32,512,128]{2,1,0:T(8,128)}) %all-gather.5.cloned.1.call-update) | async-done | bytes 8388624 | tf_op jit(solution)/shard_map/all_gather | solution.py:84
  532.5 16.9 %reshape.673 = f32[8,4,8,64,2,64]{5,4,3,2,1,0:T(2,128)} reshape(f32[32,512,128]{2,1,0:T(8,128)} %all-gather.5.cloned.1.call-done) | data formatting | bytes 16777216 | tf_op jit(solution)/shard_map/reshape | solution.py:71
  549.3 12.7 copy.47
  562.0 16.7 %gather_fusion.2 = f32[512,64,64]{2,1,0:T(8,128)} fusion(f32[8,4,8,64,2,64]{5,3,4,2,1,0:T(8,128)} %copy.57, s32[512]{0:T(512)S(1)} %reshape.657), kind=kCustom, calls=%fused_computation.2 | custom fusion | bytes 16785408 | tf_op jit(solution)/shard_map/gather | solution.py:74
  578.7 16.7 %gather_fusion.1 = f32[512,64,64]{2,1,0:T(8,128)} fusion(f32[8,4,8,64,2,64]{5,3,4,2,1,0:T(8,128)} %copy.47, s32[512]{0:T(512)S(1)} %reshape.657), kind=kCustom, calls=%fused_computation.1 | custom fusion | bytes 16785408 | tf_op jit(solution)/shard_map/gather | solution.py:74
  608.6 20.2 %copy.58 = f32[64,64,8,64]{3,2,1,0:T(8,128)} copy(f32[64,64,8,64]{3,1,2,0:T(8,128)} %bitcast.117) | data formatting | bytes 16777216 | tf_op jit(solution)/shard_map/transpose | solution.py:75
  628.8 16.5 %copy.66 = f32[64,64,8,64]{1,0,3,2:T(8,128)} copy(f32[64,64,8,64]{3,1,2,0:T(8,128)} %bitcast.119) | data formatting | bytes 16777216 | tf_op jit(solution)/shard_map/reshape | solution.py:75
  645.3 14.2 %reshape.631 = f32[4096,512]{1,0:T(8,128)} reshape(f32[64,64,8,64]{3,2,1,0:T(8,128)} %copy.58) | data formatting | bytes 16777216 | tf_op jit(solution)/shard_map/reshape | solution.py:75
  659.6 15.0 %reshape.674 = f32[4096,512]{0,1:T(8,128)} reshape(f32[64,64,8,64]{1,0,3,2:T(8,128)} %copy.66) | data formatting | bytes 16777216 | tf_op jit(solution)/shard_map/reshape | solution.py:75
  674.6 76.3 %all-reduce.9.cloned.1.call-done = (f32[512,512]{0,1:T(8,128)}, f32[512,512]{1,0:T(8,128)}) async-done(((f32[512,512]{0,1:T(8,128)}, f32[512,512]{1,0:T(8,128)}), (f32[512,512]{0,1:T(8,128)}, f32[512,512]{1,0:T(8,128)})) %all-reduce.9.cloned.1.call-update) | async-done | bytes 2097168 | tf_op jit(solution)/shard_map/psum | solution.py:13
  753.9 11.7 cholesky.103
  765.8 9.8 custom-call.34
  776.3 11.7 cholesky.215
  788.1 10.2 custom-call.35
  798.9 11.7 cholesky.236
  810.7 9.8 custom-call.36
  821.1 11.7 cholesky.253
  838.7 10.9 while.1
  849.6 40.1 %custom-call.37 = f32[4,128,128]{1,2,0:T(8,128)S(1)} custom-call(f32[4,128,128]{2,1,0:T(8,128)} %get-tuple-element.9), custom_call_target="InvertDiagBlocksLowerTriangular" | custom-call | tf_op jit(solution)/shard_map/triangular_solve | solution.py:100
  889.8 3.5 fusion.31
  893.3 3.5 convolution_subtract_fusion.4
  898.8 4.7 convolution_subtract_fusion.3
  905.5 6.7 fusion.22
  921.6 4.2 convolution_subtract_fusion.2
  925.8 3.2 fusion.69
  931.9 5.3 convolution_subtract_fusion.1
  937.2 3.3 fusion.66
  951.2 4.1 fusion.19
  955.3 3.5 fusion.65
  964.9 16.1 %multiply_subtract_fusion = f32[4096,512]{1,0:T(8,128)S(1)} fusion(f32[4096,512]{1,0:T(8,128)S(1)} %bitcast.121, f32[4096,512]{1,0:T(8,128)S(1)} %fusion.3, f32[512,512]{1,0:T(8,128)S(1)} %copy-done.13), kind=kOutput, calls=%fused_computation.16 | convolution fusion | flops 12889096192 | bytes 26214400 | tf_op jit(solution)/shard_map/dot_general | solution.py:106
  981.0 3.2 copy-done.5
  987.0 5.9 maximum_bitcast_fusion.1
  993.0 8.9 copy.61
  1001.9 48.3 %reshape.625 = f32[4,8,8,64,8,64]{5,4,3,2,1,0:T(8,128)} reshape(f32[32,512,512]{2,1,0:T(8,128)} %all-to-all-done) | data formatting | bytes 67108864 | tf_op jit(solution)/shard_map/reshape | solution.py:47
  1050.3 46.7 %copy.44 = f32[4,8,8,64,8,64]{5,3,4,2,1,0:T(8,128)} copy(f32[4,8,8,64,8,64]{5,4,3,2,1,0:T(8,128)} %reshape.625) | data formatting | bytes 67108864 | tf_op jit(solution)/shard_map/reshape | solution.py:47
  1096.9 73.9 %gather_fusion = f32[2048,64,64]{2,1,0:T(8,128)} fusion(f32[4,8,8,64,8,64]{5,3,4,2,1,0:T(8,128)} %copy.44, s32[2048]{0:T(1024)S(1)} %reshape.651), kind=kCustom, calls=%fused_computation | custom fusion | bytes 67141632 | tf_op jit(solution)/shard_map/gather | solution.py:51
  1170.8 56.3 %copy.45 = f32[64,64,32,64]{3,2,1,0:T(8,128)} copy(f32[64,64,32,64]{3,1,2,0:T(8,128)} %bitcast.3) | data formatting | bytes 67108864 | tf_op jit(solution)/shard_map/transpose | solution.py:59
  1227.2 56.4 %reshape.626 = f32[4096,2048]{1,0:T(8,128)} reshape(f32[64,64,32,64]{3,2,1,0:T(8,128)} %copy.45) | data formatting | bytes 67108864 | tf_op jit(solution)/shard_map/reshape | solution.py:59
  1283.6 116.2 %convolution_subtract_fusion = f32[4096,2048]{1,0:T(8,128)} fusion(f32[4096,2048]{1,0:T(8,128)} %reshape.626, f32[4096,512]{1,0:T(8,128)} %copy-done.5, f32[4096,512]{1,0:T(8,128)} %copy-done, f32[2048,512]{1,0:T(8,128)} %get-tuple-element.26, f32[2048,512]{1,0:T(8,128)} %get-tuple-element.27), kind=kOutput, calls=%fused_computation.6 | convolution fusion | flops 103093895168 | bytes 92274688 | tf_op jit(solution)/shard_map/dot_general | solution.py:115
  (126 shorter events, 73.4 us)
Async XLA Ops:
  9.4 41.7 %all-to-all-start.2 = ((f32[4,512,128]{2,1,0:T(8,128)}), f32[4,512,128]{2,1,0:T(8,128)S(1)}, u32[]{:S(2)}, u32[]{:S(2)}) async-start(f32[4,512,128]{2,1,0:T(8,128)} %bitcast.22), calls=%async_computation.2 | async-start | bytes 2097152 | tf_op jit(solution)/shard_map/all_to_all | solution.py:81
  51.2 16.3 %copy-start.11 = (f32[4,512,128]{2,1,0:T(8,128)}, f32[4,512,128]{2,1,0:T(8,128)S(1)}, u32[]{:S(2)}) copy-start(f32[4,512,128]{2,1,0:T(8,128)S(1)} %all-to-all-done.2) | copy-start | bytes 3145732
  51.2 52.7 %all-to-all-start.1 = ((f32[4,512,128]{2,1,0:T(8,128)}), f32[4,512,128]{2,1,0:T(8,128)S(1)}, u32[]{:S(2)}, u32[]{:S(2)}) async-start(f32[4,512,128]{2,1,0:T(8,128)} %bitcast.4), calls=%async_computation.1 | async-start | bytes 2097152 | tf_op jit(solution)/shard_map/all_to_all | solution.py:80
  103.8 1.0 copy-start.12
  103.8 10.4 copy-start.14
  103.8 10.5 copy-start.15
  104.8 897.1 %all-to-all-start = ((f32[32,512,512]{2,1,0:T(8,128)}), f32[32,512,512]{2,1,0:T(8,128)}, u32[]{:S(2)}, u32[]{:S(2)}) async-start(f32[32,512,512]{2,1,0:T(8,128)} %bitcast.114), calls=%async_computation | async-start | bytes 67108864 | tf_op jit(solution)/shard_map/all_to_all | solution.py:40
  112.2 179.5 %all-gather.7.cloned.1.call-start = ((), (), s32[]{:S(2)}) async-start(), calls=%async_computation.4 | async-start | bytes 9437184 | tf_op jit(solution)/shard_map/all_gather | solution.py:85
  112.9 419.5 %all-gather.5.cloned.1.call-start = ((), (), s32[]{:S(2)}) async-start(), calls=%async_computation.3 | async-start | bytes 9437184 | tf_op jit(solution)/shard_map/all_gather | solution.py:84
  113.7 637.2 %all-reduce.9.cloned.1.call-start = ((), (), s32[]{:S(2)}) async-start(), calls=%async_computation.6 | async-start | bytes 4194304 | tf_op jit(solution)/shard_map/psum | solution.py:13
  606.6 677.0 %all-reduce.7.cloned.1.call-start = ((), (), s32[]{:S(2)}) async-start(), calls=%async_computation.5 | async-start | bytes 16777216 | tf_op jit(solution)/shard_map/psum | solution.py:13
  898.8 6.7 copy-start.2
  905.5 6.7 copy-start.4
  914.2 1.3 copy-start.7
  943.5 7.6 copy-start.1
  943.6 7.6 copy-start.3
  943.6 7.6 copy-start.6
  951.2 7.6 copy-start.8
  951.2 7.6 copy-start.9
  951.2 7.6 copy-start.10
  955.3 9.6 slice-start
  958.9 6.0 slice-start.1
  960.3 4.5 copy-start
  960.4 4.5 copy-start.13
  981.0 3.2 copy-start.5
Sparse Core Ops, SparseCore 0:
  115.2 176.4 all-gather.6
  293.3 239.1 all-gather.4
  606.8 144.1 all-reduce.8
  986.8 170.1 all-reduce.6
where the time goes:
time: 1420 us; the launch traced here: 1410 us
  local copies, waits for them, and re-layouts  574 us (40%)
  waiting for transfers between devices  465 us (33%)
  matrix products  193 us (14%)
  other arithmetic  141 us (10%)
  between operations  17.4 us (1%)
  starting transfers between devices  15.4 us (1%)
    all_gather x1, waiting for transfers between devices, per_device(): lax.all_gather(s_rows[None], 'col', axis=0, tiled=True)  211 us
    all_gather x1, waiting for transfers between devices, per_device(): lax.all_gather(h_rows[None], 'col', axis=0, tiled=True)  177 us
    dot_general x1, matrix products, per_device(): lax.dot_general(left_terms, right_terms, (((1,), (1,)), ((), ())), precis...  116 us
    reshape x2, local copies, waits for them, and re-layouts, per_device(): received.reshape(row_count, col_count, rounds_row, BLOCK, rounds_col, BLOCK)  95 us
    another operation x15, other arithmetic, per_device(): lower_factor = jnp.linalg.cholesky(corner_s)  79.6 us
    psum x2, waiting for transfers between devices, broadcast(): return lax.psum(block, axis)  76.3 us
    gather x1, local copies, waits for them, and re-layouts, per_device(): grid_h[source_row, source_col, jnp.broadcast_to(round_row, shape_two), :,...  73.9 us
    reshape x4, local copies, waits for them, and re-layouts, arrange(): gathered.reshape(col_count, row_count, rounds_row, BLOCK, panel_local //...  59.8 us
  transfers between devices with their start and end apart: 7, of which 3 were waited for; matrix products, arithmetic and copies ran while one was open for 56% of the time, Pallas kernels for 0%

commit v1 on v0

v1 whole, which is shorter than its diff:
```python
import functools

import jax
import jax.numpy as jnp
from jax import lax
from jax.experimental import pallas as pl
from jax.experimental.pallas import tpu as pltpu
from jax.sharding import PartitionSpec as P

ORDER = 16384
PANEL = 512
BLOCK = 64
HIGHEST = lax.Precision.HIGHEST


def pack_kernel(in_ref, out_ref):
    out_ref[0] = in_ref[...]


def pack(local, row_count, col_count):
    rows, cols = local.shape
    part_rows, part_cols = rows // row_count, cols // col_count
    return pl.pallas_call(
        pack_kernel,
        grid=(row_count, col_count),
        in_specs=[pl.BlockSpec((part_rows, part_cols), lambda i, j: (i, j))],
        out_specs=pl.BlockSpec(
            (1, part_rows, part_cols), lambda i, j: (i * col_count + j, 0, 0)
        ),
        out_shape=jax.ShapeDtypeStruct((row_count * col_count, part_rows, part_cols), local.dtype),
        cost_estimate=pl.CostEstimate(
            flops=0, bytes_accessed=2 * local.size * 4, transcendentals=0
        ),
        name="pack",
    )(local)


def panel_kernel(old_rows, old_cols, panel_local, panel_blocks, dev_row, dev_col, in_ref, s_ref, h_ref):
    group = pl.program_id(0)
    for gi in range(old_rows):
        row_part = dev_row[group * old_rows + gi]
        rows = pl.ds(gi * BLOCK, BLOCK)
        for base, out_ref in ((0, s_ref), (panel_local, h_ref)):
            for k in range(0, panel_blocks, 2):
                pair = []
                for kk in (k, k + 1):
                    start = base + kk // old_cols * BLOCK
                    pair.append(in_ref[row_part + dev_col[kk], :, start : start + BLOCK])
                out_ref[rows, k * BLOCK : (k + 2) * BLOCK] = jnp.concatenate(pair, axis=1)


def arrange_panel(gathered, dev_row, dev_col, old_rows, old_cols, panel_local):
    devices, part_rows, width = gathered.shape
    groups = part_rows // BLOCK
    height = old_rows * BLOCK
    shape = jax.ShapeDtypeStruct((groups * height, PANEL), jnp.float32)
    out_spec = pl.BlockSpec((height, PANEL), lambda g, *_: (g, 0))
    return pl.pallas_call(
        functools.partial(panel_kernel, old_rows, old_cols, panel_local, PANEL // BLOCK),
        grid_spec=pltpu.PrefetchScalarGridSpec(
            num_scalar_prefetch=2,
            grid=(groups,),
            in_specs=[pl.BlockSpec((devices, BLOCK, width), lambda g, *_: (0, g, 0))],
            out_specs=[out_spec, out_spec],
        ),
        out_shape=[shape, shape],
        cost_estimate=pl.CostEstimate(
            flops=0, bytes_accessed=2 * gathered.size * 4, transcendentals=0
        ),
        name="arrange_panel",
    )(dev_row, dev_col, gathered)


def split(x):
    high = x.astype(jnp.bfloat16)
    return high, (x - high.astype(jnp.float32)).astype(jnp.bfloat16)


def update_kernel(
    old_rows,
    old_cols,
    rounds_col,
    dev_row,
    dev_col,
    in_ref,
    left_n,
    left_q,
    right_q,
    right_n,
    out_ref,
    left_hi,
    left_lo,
    right_hi,
    right_lo,
):
    group = pl.program_id(0)

    @pl.when(group == 0)
    def _():
        right_hi[:, :PANEL], right_lo[:, :PANEL] = split(right_q[...])
        right_hi[:, PANEL:], right_lo[:, PANEL:] = split(right_n[...])

    left_hi[:, :PANEL], left_lo[:, :PANEL] = split(left_n[...])
    left_hi[:, PANEL:], left_lo[:, PANEL:] = split(left_q[...])
    span = 2 * old_cols * BLOCK

    def chunk(t, carry):
        cols = pl.ds(pl.multiple_of(t * span, span), span)
        dims = (((1,), (1,)), ((), ()))

        def product(a, b):
            return lax.dot_general(
                a[...], b[cols, :], dims, preferred_element_type=jnp.float32
            )

        update = (
            product(left_hi, right_lo) + product(left_lo, right_hi)
        ) + product(left_hi, right_hi)
        lanes = pl.ds(pl.multiple_of(t * 2 * BLOCK, 2 * BLOCK), 2 * BLOCK)
        for gi in range(old_rows):
            row_part = dev_row[group * old_rows + gi]
            top = gi * BLOCK
            for k in range(0, 2 * old_cols, 2):
                start = k // old_cols * BLOCK
                pair = []
                for kk in (k, k + 1):
                    device = row_part + dev_col[t * 2 * old_cols + kk]
                    pair.append(in_ref[device, :, lanes][:, start : start + BLOCK])
                block = jnp.concatenate(pair, axis=1)
                where = pl.ds(
                    pl.multiple_of(t * span + k * BLOCK, 2 * BLOCK), 2 * BLOCK
                )
                out_ref[top : top + BLOCK, where] = (
                    block - update[top : top + BLOCK, k * BLOCK : (k + 2) * BLOCK]
                )
        return carry

    lax.fori_loop(0, rounds_col // 2, chunk, 0)


def assemble_and_update(received, coupling, mixed, column_q, column_n, dev_row, dev_col, old_rows, old_cols):
    devices, part_rows, part_cols = received.shape
    groups = part_rows // BLOCK
    height = old_rows * BLOCK
    band = groups * height
    strip = column_q.shape[0]
    left_spec = pl.BlockSpec((height, PANEL), lambda g, *_: (g, 0))
    right_spec = pl.BlockSpec(
        (strip, PANEL), lambda g, *_: (0, 0), pipeline_mode=pl.Buffered(1)
    )
    return pl.pallas_call(
        functools.partial(update_kernel, old_rows, old_cols, part_cols // BLOCK),
        grid_spec=pltpu.PrefetchScalarGridSpec(
            num_scalar_prefetch=2,
            grid=(groups,),
            in_specs=[
                pl.BlockSpec((devices, BLOCK, part_cols), lambda g, *_: (0, g, 0)),
                left_spec,
                left_spec,
                right_spec,
                right_spec,
            ],
            out_specs=pl.BlockSpec((height, strip), lambda g, *_: (g, 0)),
            scratch_shapes=[
                pltpu.VMEM((height, 2 * PANEL), jnp.bfloat16),
                pltpu.VMEM((height, 2 * PANEL), jnp.bfloat16),
                pltpu.VMEM((strip, 2 * PANEL), jnp.bfloat16),
                pltpu.VMEM((strip, 2 * PANEL), jnp.bfloat16),
            ],
        ),
        out_shape=jax.ShapeDtypeStruct((band, strip), jnp.float32),
        cost_estimate=pl.CostEstimate(
            flops=3 * 4 * band * strip * PANEL,
            bytes_accessed=2 * received.size * 4,
            transcendentals=0,
        ),
        name="assemble_and_update",
    )(dev_row, dev_col, received, coupling, mixed, column_q, column_n)


def broadcast(block, axis, holder):
    block = jnp.where(lax.axis_index(axis) == holder, block, jnp.zeros_like(block))
    return lax.psum(block, axis)


def per_device(h_old, s_old, row_owner, col_owner):
    row_count = lax.axis_size("row")
    col_count = lax.axis_size("col")
    old_rows = 2 * row_count
    old_cols = col_count // 2
    row_id = lax.axis_index("row")
    col_id = lax.axis_index("col")
    local_h = h_old[0, 0]
    local_s = s_old[0, 0]
    rows_here, cols_here = local_h.shape
    part_rows = rows_here // row_count
    part_cols = cols_here // col_count
    band = ORDER // row_count
    strip = ORDER // col_count
    panel_local = local_s.shape[1]
    span_row = part_rows // BLOCK * old_rows
    span_col = part_cols // BLOCK * old_cols
    panel_blocks = PANEL // BLOCK
    owner_row = lax.dynamic_slice_in_dim(row_owner, row_id * span_row, span_row)
    owner_col = lax.dynamic_slice_in_dim(col_owner, col_id * span_col, span_col)

    panels = jnp.concatenate([local_s, local_h[:, :panel_local]], 1)
    corner_rows = -(-panel_blocks // old_rows) * BLOCK
    corners = lax.all_gather(panels[:corner_rows][None], ("row", "col"), axis=0, tiled=True)
    corner_owner = row_owner[: corner_rows // BLOCK * old_rows]
    panel_col = 2 * col_owner[:panel_blocks]
    corner_s, corner_h = arrange_panel(
        corners,
        corner_owner // 2 * col_count + corner_owner % 2,
        panel_col,
        old_rows,
        old_cols,
        panel_local,
    )
    corner_s, corner_h = corner_s[:PANEL], corner_h[:PANEL]

    pieces = panels.reshape(row_count, part_rows, 2 * panel_local)
    rows = lax.all_to_all(pieces, "row", split_axis=0, concat_axis=0, tiled=True)
    gathered = lax.all_gather(rows, "col", axis=0, tiled=True)
    s_panel, h_panel = arrange_panel(
        gathered,
        owner_row % 2 * row_count + owner_row // 2,
        panel_col * row_count,
        old_rows,
        old_cols,
        panel_local,
    )

    received = lax.all_to_all(
        pack(local_h, row_count, col_count),
        ("row", "col"),
        split_axis=0,
        concat_axis=0,
        tiled=True,
    )

    lower_factor = jnp.linalg.cholesky(corner_s)
    identity = jnp.eye(PANEL, dtype=jnp.float32)
    inverse = lax.linalg.triangular_solve(lower_factor, identity, left_side=True, lower=True)
    panel_factor = lax.dot_general(
        s_panel, inverse, (((1,), (1,)), ((), ())), precision=HIGHEST
    )
    coupling = jnp.dot(panel_factor, inverse, precision=HIGHEST)
    top_rows = jnp.concatenate(
        [identity - inverse, jnp.zeros((band - PANEL, PANEL), jnp.float32)], 0
    )
    leading = jnp.logical_and(row_id == 0, jnp.arange(band, dtype=jnp.int32)[:, None] < PANEL)
    coupling = jnp.where(leading, top_rows, coupling)
    mixed = h_panel - 0.5 * jnp.dot(coupling, corner_h, precision=HIGHEST)
    offset = col_id * strip % band
    root_row = col_id * strip // band
    column_n, column_q = (
        broadcast(lax.dynamic_slice_in_dim(coupling, offset, strip), "row", root_row),
        broadcast(lax.dynamic_slice_in_dim(mixed, offset, strip), "row", root_row),
    )
    h_reduced = assemble_and_update(
        received,
        coupling,
        mixed,
        column_q,
        column_n,
        owner_row // 2 * col_count + owner_row % 2,
        2 * owner_col,
        old_rows,
        old_cols,
    )
    return (h_reduced, panel_factor)


def solution(mesh):
    in_specs = (P("row", "col", None, None), P("row", "col", None, None), P(), P())
    out_specs = (P("row", "col"), P("row", None))
    return jax.shard_map(
        per_device, mesh=mesh, in_specs=in_specs, out_specs=out_specs, check_vma=False
    )
```

time: 1420 us -> 1080 us (0.76)
  local copies, waits for them, and re-layouts: 574 us -> 17.2 us
  waiting for transfers between devices: 465 us -> 713 us
  matrix products: 193 us -> 54.5 us
  Pallas kernels: 0 us -> 127 us
    reshape x10 -> x0, local copies, waits for them, and re-layouts: 257 us -> none  [the longest x2 95 us: per_device(): received.reshape(row_count, col_count, rounds_row, BLOCK, rounds_col, BLOCK)]
    psum x2 -> x1, waiting for transfers between devices: 76.3 us -> 292 us  [broadcast(): return lax.psum(block, axis)]
    pallas_call x0 -> x4, Pallas kernels: none -> 127 us  [the longest x1 72.1 us: assemble_and_update(): pl.pallas_call(functools.partial(update_kernel, old_rows, old_cols, part_...]
    transpose x4 -> x0, local copies, waits for them, and re-layouts: 126 us -> none  [the longest x1 56.3 us: per_device(): h_block = picked.transpose(0, 2, 1, 3).reshape(band, strip)]
    gather x3 -> x0, local copies, waits for them, and re-layouts: 107 us -> none  [the longest x1 73.9 us: per_device(): grid_h[source_row, source_col, jnp.broadcast_to(round_row, shape_two), :,...]
    dot_general x2 -> x3, matrix products: 132 us -> 48.9 us  [the longest x1 17.2 us: per_device(): lax.dot_general(s_panel, inverse, (((1,), (1,)), ((), ())), precision=HIG...]
    another operation x14 -> x0, matrix products: 51.1 us -> none  [the longest x7 26.7 us: per_device(): lax.linalg.triangular_solve(lower_factor, solved, left_side=True, lower=T...]
    unnamed x38 -> x18, local copies, waits for them, and re-layouts: 54.5 us -> 4.54 us
  transfers between devices with their start and end apart: 7 -> 5, of which waited for: 3 -> 3; matrix products, arithmetic and copies ran while one was open for 56% -> 18% of each run, Pallas kernels for 0% -> 5%
where the time goes in v1:
time: 1080 us; the launch traced here: 1070 us
  waiting for transfers between devices  713 us (66%)
  other arithmetic  134 us (12%)
  Pallas kernels  127 us (12%)
  matrix products  54.5 us (5%)
  local copies, waits for them, and re-layouts  17.2 us (2%)
  between operations  16.8 us (2%)
    psum x1, waiting for transfers between devices, broadcast(): return lax.psum(block, axis)  292 us
    all_gather x1, waiting for transfers between devices, per_device(): lax.all_gather(panels[:corner_rows][None], ('row', 'col'), axis=0, tiled=...  231 us
    all_gather x1, waiting for transfers between devices, per_device(): gathered = lax.all_gather(rows, 'col', axis=0, tiled=True)  189 us
    another operation x14, other arithmetic, per_device(): lower_factor = jnp.linalg.cholesky(corner_s)  78.8 us
    pallas_call x1, Pallas kernels, assemble_and_update(): pl.pallas_call(functools.partial(update_kernel, old_rows, old_cols, part_...  72.1 us
    another operation x3, other arithmetic, per_device(): lax.linalg.triangular_solve(lower_factor, identity, left_side=True, lower...  40.3 us
    pallas_call x1, Pallas kernels, pack(): pl.pallas_call(pack_kernel, grid=(row_count, col_count), in_specs=[pl.Blo...  34.4 us
  transfers between devices with their start and end apart: 5, of which 3 were waited for; matrix products, arithmetic and copies ran while one was open for 18% of the time, Pallas kernels for 5%

profile of v1, /device:TPU:11, one launch (start us, length us, event | category | flops | bytes accessed | tf_op | source)
XLA Modules:
  0.0 1072.2 jit_solution(2503307395857276689)
XLA Ops:
  7.2 1.3 slice.130
  8.5 2.7 pad_maximum_fusion
  11.1 3.8 all-to-all-start.1
  15.0 34.4 %pack.1 = f32[32,512,512]{2,1,0:T(8,128)} custom-call(f32[2048,4096]{1,0:T(8,128)} %bitcast.58), custom_call_target="tpu_custom_call" | custom-call | bytes 67108864 | tf_op jit(solution)/shard_map/pack/pallas_call | solution.py:23
  49.4 1.3 copy-done.3
  50.7 6.7 all-to-all-start
  57.5 1.4 pad_maximum_fusion.4
  59.0 0.7 all-gather.4.cloned.1.call-update
  59.8 0.7 multiply_add_fusion
  60.5 0.8 iota_compare_fusion.1
  61.4 0.6 fusion.31.dev_row
  62.0 0.6 slice_multiply_fusion
  62.5 231.4 %all-gather.6.cloned.1.call-done = f32[2048,256]{1,0:T(8,128)} async-done(((f32[64,256]{1,0:T(8,128)}), f32[2048,256]{1,0:T(8,128)}) %all-gather.6.cloned.1.call-update) | async-done | bytes 2097168 | tf_op jit(solution)/shard_map/all_gather | solution.py:209
  293.9 4.2 arrange_panel.2
  298.1 1.6 copy.7
  299.6 1.4 fusion
  301.1 11.7 %cholesky.104 = f32[128,128]{1,0:T(8,128)S(1)} custom-call(f32[128,128]{1,0:T(8,128)S(1)} %cholesky.266), custom_call_target="Cholesky" | custom-call | tf_op jit(solution)/shard_map/jit(cholesky)/cholesky | solution.py:242
  313.0 9.8 custom-call.30
  323.5 11.7 %cholesky.217 = f32[128,128]{1,0:T(8,128)S(1)} custom-call(f32[128,128]{1,0:T(8,128)S(1)} %cholesky.270), custom_call_target="Cholesky" | custom-call | tf_op jit(solution)/shard_map/jit(cholesky)/cholesky | solution.py:242
  335.2 10.0 custom-call.31
  345.8 11.7 %cholesky.238 = f32[128,128]{1,0:T(8,128)S(1)} custom-call(f32[128,128]{1,0:T(8,128)S(1)} %cholesky.275), custom_call_target="Cholesky" | custom-call | tf_op jit(solution)/shard_map/jit(cholesky)/cholesky | solution.py:242
  357.6 9.8 custom-call.32
  368.0 12.1 %cholesky.255 = f32[128,128]{1,0:T(8,128)S(1)} custom-call(f32[128,128]{1,0:T(8,128)S(1)} %convolution_subtract_fusion.5), custom_call_target="Cholesky" | custom-call | tf_op jit(solution)/shard_map/jit(cholesky)/cholesky | solution.py:242
  380.1 0.6 compare_reduce_fusion.2
  381.9 0.6 compare_reduce_fusion.1
  383.1 0.6 compare_reduce_fusion
  384.4 9.7 while.1
  384.5 0.5 fusion.47
  385.0 1.8 bitcast_dynamic-update-slice_fusion.2
  387.4 1.8 bitcast_dynamic-update-slice_fusion.2
  389.3 0.5 fusion.47
  389.8 1.8 bitcast_dynamic-update-slice_fusion.2
  392.3 1.8 bitcast_dynamic-update-slice_fusion.2
  394.1 40.1 %custom-call.33 = f32[4,128,128]{1,2,0:T(8,128)S(1)} custom-call(f32[4,128,128]{2,1,0:T(8,128)} %get-tuple-element.17), custom_call_target="InvertDiagBlocksLowerTriangular" | custom-call | tf_op jit(solution)/shard_map/triangular_solve | solution.py:244
  434.2 1.1 fusion.11
  437.0 0.6 convolution_subtract_fusion.2
  438.2 188.7 %all-gather.4.cloned.1.call-done.in_ref = f32[32,512,256]{2,1,0:T(8,128)} async-done(((f32[4,512,256]{2,1,0:T(8,128)}), f32[32,512,256]{2,1,0:T(8,128)}) %all-gather.4.cloned.1.call-update) | async-done | bytes 16777232 | tf_op jit(solution)/shard_map/all_gather | solution.py:224
  626.9 16.0 %arrange_panel.3 = (f32[4096,512]{1,0:T(8,128)}, f32[4096,512]{1,0:T(8,128)}) custom-call(s32[64]{0:T(128)} %get-tuple-element.28.dev_row, s32[8]{0:T(128)} %get-tuple-element.43.dev_col, f32[32,512,256]{2,1,0:T(8,128)} %all-gather.4.cloned.1.call-done.in_ref), custom_call_target="tpu_custom_call" | custom-call | bytes 33554432 | tf_op jit(solution)/shard_map/arrange_panel/pallas_call | solution.py:58
  642.9 17.2 %fusion.17 = f32[4096,512]{1,0:T(8,128)S(1)} fusion(f32[4096,512]{1,0:T(8,128)} %get-tuple-element.7, f32[128,512]{1,0:T(8,128)S(1)} %fusion.21, f32[128,512]{1,0:T(8,128)S(1)} %fusion.22, f32[128,512]{1,0:T(8,128)S(1)} %fusion.24, f32[128,512]{1,0:T(8,128)S(1)} %fusion.11), kind=kOutput, calls=%fused_computation.38 | convolution fusion | flops 12885688320 | bytes 17825792 | tf_op jit(solution)/shard_map/dot_general | solution.py:245
  660.1 15.6 %pad_select_fusion.left_n = f32[4096,512]{1,0:T(8,128)S(1)} fusion(f32[512,512]{1,0:T(8,128)S(1)} %convert_subtract_fusion, f32[4096,512]{1,0:T(8,128)S(1)} %fusion.17, pred[4096]{0:T(1024)(128)(4,1)S(1)} %fusion.30, f32[128,512]{1,0:T(8,128)S(1)} %fusion.21, f32[128,512]{1,0:T(8,128)S(1)} %fusion.22, f32[128,512]{1,0:T(8,128)S(1)} %fusion.24, ...), kind=kOutput, calls=%fused_computation.3 | convolution fusion | flops 12887785472 | bytes 18878464 | tf_op jit(solution)/shard_map/dot_general | solution.py:248
  675.8 2.5 dynamic-slice_select_fusion
  678.3 16.0 %multiply_subtract_fusion.left_q = f32[4096,512]{1,0:T(8,128)S(1)} fusion(f32[4096,512]{1,0:T(8,128)S(1)} %bitcast.60, f32[4096,512]{1,0:T(8,128)S(1)} %pad_select_fusion.left_n, f32[512,512]{1,0:T(8,128)S(1)} %copy-done.4), kind=kOutput, calls=%fused_computation.2 | convolution fusion | flops 12889096192 | bytes 26214400 | tf_op jit(solution)/shard_map/dot_general | solution.py:254
  694.3 3.2 copy-done.2
  697.5 2.4 dynamic-slice_select_fusion.1
  700.0 0.6 dynamic-slice_multiply_fusion.dev_col
  700.6 0.5 multiply_add_fusion.1.dev_row
  701.2 292.0 %all-reduce.5.cloned.1.call-done = (f32[2048,512]{1,0:T(8,128)}, f32[2048,512]{1,0:T(8,128)}) async-done(((f32[2048,512]{1,0:T(8,128)}, f32[2048,512]{1,0:T(8,128)}), (f32[2048,512]{1,0:T(8,128)}, f32[2048,512]{1,0:T(8,128)})) %all-reduce.5.cloned.1.call-update) | async-done | bytes 8388624 | tf_op jit(solution)/shard_map/psum | solution.py:183
  993.2 72.1 %assemble_and_update.1 = f32[4096,2048]{1,0:T(8,128)} custom-call(s32[64]{0:T(128)} %multiply_add_fusion.1.dev_row, s32[32]{0:T(128)} %dynamic-slice_multiply_fusion.dev_col, f32[32,512,512]{2,1,0:T(8,128)} %all-to-all-done.in_ref, f32[4096,512]{1,0:T(8,128)} %copy-done, f32[4096,512]{1,0:T(8,128)} %copy-done.2, f32[2048,512]{1,0:T(8,128)} %get-tuple-element.26.right_q, ...), custom_call_target="tpu_custom_call" | custom-call | flops 51539607552 | bytes 67108864 | tf_op jit(solution)/shard_map/assemble_and_update/pallas_call | solution.py:151
  (56 shorter events, 6.1 us)
Async XLA Ops:
  11.1 38.3 %all-to-all-start.1 = ((f32[4,512,256]{2,1,0:T(8,128)}), f32[4,512,256]{2,1,0:T(8,128)S(1)}, u32[]{:S(2)}, u32[]{:S(2)}) async-start(f32[4,512,256]{2,1,0:T(8,128)} %pad_maximum_fusion), calls=%async_computation.1 | async-start | bytes 4194304 | tf_op jit(solution)/shard_map/all_to_all | solution.py:223
  49.4 1.3 copy-start.3
  49.4 10.4 copy-start.5
  49.4 12.5 %copy-start.6 = (s32[256]{0:T(256)S(1)}, s32[256]{0:T(256)}, u32[]{:S(2)}) copy-start(s32[256]{0:T(256)} %param.7) | copy-start | bytes 3076
  50.7 942.5 %all-to-all-start = ((f32[32,512,512]{2,1,0:T(8,128)}), f32[32,512,512]{2,1,0:T(8,128)}, u32[]{:S(2)}, u32[]{:S(2)}) async-start(f32[32,512,512]{2,1,0:T(8,128)} %pack.1), calls=%async_computation | async-start | bytes 67108864 | tf_op jit(solution)/shard_map/all_to_all | solution.py:234
  57.4 236.5 %all-gather.6.cloned.1.call-start = ((), (), s32[]{:S(2)}) async-start(), calls=%async_computation.3 | async-start | bytes 2162688 | tf_op jit(solution)/shard_map/all_gather | solution.py:209
  58.9 568.0 %all-gather.4.cloned.1.call-start = ((), (), s32[]{:S(2)}) async-start(), calls=%async_computation.2 | async-start | bytes 18874368 | tf_op jit(solution)/shard_map/all_gather | solution.py:224
  59.7 933.5 %all-reduce.5.cloned.1.call-start = ((), (), s32[]{:S(2)}) async-start(), calls=%async_computation.4 | async-start | bytes 16777216 | tf_op jit(solution)/shard_map/psum | solution.py:183
  642.9 35.4 %slice-start = ((s8[8388608]{0:T(1024)(128)(4,1)}), s8[4194304]{0:T(1024)(128)(4,1)S(1)}, s32[]{:S(2)}) async-start(s8[8388608]{0:T(1024)(128)(4,1)} %bitcast.59), calls=%async_computation.5 | async-start | bytes 8388608
  660.1 15.7 %copy-start.1 = (f32[4096,512]{1,0:T(8,128)}, f32[4096,512]{1,0:T(8,128)S(1)}, u32[]{:S(2)}) copy-start(f32[4096,512]{1,0:T(8,128)S(1)} %fusion.17) | copy-start | bytes 25165828
  660.1 18.2 %slice-start.1 = ((s8[8388608]{0:T(1024)(128)(4,1)}), s8[4194304]{0:T(1024)(128)(4,1)S(1)}, s32[]{:S(2)}) async-start(s8[8388608]{0:T(1024)(128)(4,1)} %bitcast.59), calls=%async_computation.6 | async-start | bytes 8388608
  675.8 18.5 %copy-start = (f32[4096,512]{1,0:T(8,128)}, f32[4096,512]{1,0:T(8,128)S(1)}, u32[]{:S(2)}) copy-start(f32[4096,512]{1,0:T(8,128)S(1)} %pad_select_fusion.left_n) | copy-start | bytes 25165828
  675.8 2.5 copy-start.4
  694.3 3.2 copy-start.2
Sparse Core Ops, SparseCore 0:
  61.2 232.6 all-gather.5
  296.1 330.7 all-gather.3
  700.1 293.0 all-reduce.4
